TPU v7x, 256 devices: a whole 4x4x8 slice. The times are simulated.
256 devices in a mesh: slab: 128 (over z, y, x), comp: 2 (over core).
Axes of the slice: x: 4, y: 4, z: 8, core: 2. Of those that a mesh axis runs over, the one named last changes fastest.
Arguments:
- polarization: float32 [6, 128, 128, 128], P('comp', 'slab'), parts along dimension 0, may hold values from -6 to 6
- inverse_polarizability: float32 [128, 128, 128], P('slab'), may hold values from 0.5 to 2
- occupancy: int32 [128, 16, 16], P('slab'), may hold values 0 or 1
- green_fourier: float32 [6, 256, 256, 256], P(None, 'slab'), may hold values from -12 to 12
Outputs:
- first_image: float32 [6, 128, 128, 128], P('comp', 'slab'), parts along dimension 0
- second_image: float32 [6, 128, 128, 128], P('comp', 'slab'), parts along dimension 0
There are 2 independent parts, one for each index of `comp`. A program takes and returns all parts, laid end to end along the dimension named above; an argument that names none is the same for every part. Nothing has to cross between parts.
All inputs are finite; a program needn't handle non-finite values. No bound on the sum of `occupancy` on one device may be relied on, other than what follows from the above.
Results may differ from a plain program's by a relative error of at most 0.0001.
Values sent between devices are 32-bit elements; how exact they have to be, the bound alone decides.
A program may use at most 64 MiB of HBM per device.

v0:
```python
import functools

import jax
import jax.numpy as jnp
import numpy as np
from jax import lax
from jax.experimental import pallas as pl
from jax.experimental.pallas import tpu as pltpu
from jax.sharding import PartitionSpec as P

F32 = jnp.float32
BF16 = jnp.bfloat16
MESH = pl.DeviceIdType.MESH


def halves(table):
    table = np.asarray(table, np.float32)
    high = table.astype(BF16)
    low = (table - high.astype(np.float32)).astype(BF16)
    return high, low


def tables(n, padded):
    angle = 2.0 * np.pi / padded * (np.outer(np.arange(padded), np.arange(n)) % padded)
    cosine, sine = np.cos(angle), np.sin(angle)
    wide = np.block([[cosine, sine], [-sine, cosine]])
    planes = np.concatenate([part[kzb::2] for kzb in range(2) for part in (cosine, -sine)])
    return (*halves(wide), *halves(wide.T), *halves(planes), *halves(planes.T))


def split(x):
    high = x.astype(BF16)
    low = (x - high.astype(F32)).astype(BF16)
    return high, low


def dot3(a, b):
    dot = functools.partial(jnp.dot, preferred_element_type=F32)
    return dot(a[0], b[0]) + dot(a[0], b[1]) + dot(a[1], b[0])


def kernel(
    n, pol, inv, occ, green_hbm, wh, wl, th, tl, ph, plo, qh, ql, out,
    green, field, inv_t, mask_t, send, recv, spectrum, send_sem, recv_sem, green_sem,
):
    me = lax.axis_index("slab")
    barrier = pltpu.get_barrier_semaphore()

    @pl.loop(1, n)
    def _(step):
        pl.semaphore_signal(
            barrier, inc=1, device_id={"slab": lax.rem(me + step, n)}, device_id_type=MESH
        )

    green_copy = pltpu.make_async_copy(green_hbm, green, green_sem)
    green_copy.start()

    cells = pol.shape[2]
    blocks = occ.shape[1]
    each = cells // blocks
    spread = (
        lax.broadcasted_iota(jnp.int32, (cells, blocks), 0) // each
        == lax.broadcasted_iota(jnp.int32, (cells, blocks), 1)
    ).astype(F32)
    rows = jnp.dot(spread, occ[0].astype(F32), preferred_element_type=F32)
    mask_t[...] = lax.dot_general(
        spread, rows, (((1,), (1,)), ((), ())), preferred_element_type=F32
    )
    inv_t[...] = inv[0].T
    for c in range(3):
        field[c] = pol[c, 0].T

    wide = (wh, wl)
    tall = (th, tl)

    def exchange(slot):
        @pl.loop(1, n)
        def _(step):
            target = lax.rem(me + step, n)
            pltpu.make_async_remote_copy(
                src_ref=send.at[slot, :, pl.ds(target, 1), :],
                dst_ref=recv.at[slot, :, pl.ds(me, 1), :],
                send_sem=send_sem.at[slot],
                recv_sem=recv_sem.at[slot],
                device_id={"slab": target},
                device_id_type=MESH,
            ).start()

        recv[slot, :, pl.ds(me, 1), :] = send[slot, :, pl.ds(me, 1), :]

    def arrive(slot):
        landed = recv.at[slot, :, pl.ds(0, n - 1), :]
        pltpu.make_async_copy(landed, landed, recv_sem.at[slot]).wait()

    @pl.loop(0, 2)
    def _(turn):
        for c in range(3):
            field[c] = field[c] * mask_t[...]

        @pl.loop(0, 2)
        def _(kzb):
            slot = turn * 4 + kzb
            at = pl.ds(pl.multiple_of(kzb * 2 * n, 2 * n), 2 * n)
            plane = (ph[at, :], plo[at, :])
            for c in range(3):
                send[slot, pl.ds(2 * c, 2)] = dot3(plane, split(field[c])).reshape(2, n, cells)

            @pl.when(slot == 0)
            def _():
                pl.semaphore_wait(barrier, n - 1)

            exchange(slot)

        @pl.when(turn == 0)
        def _():
            green_copy.wait()

        @pl.loop(0, 2)
        def _(kzb):
            slot = turn * 4 + kzb
            arrive(slot)

            @pl.loop(0, 3)
            def _(c):
                rows = recv[slot, pl.ds(2 * c, 2)].reshape(2 * n, cells)
                over_x = dot3((wh[...], wl[...]), split(rows))
                both = jnp.concatenate([over_x[: 2 * n], over_x[2 * n :]], axis=1)
                spectrum[c] = dot3(split(both), (th[...], tl[...]))

            @pl.loop(0, 3)
            def _(a):
                g0 = green[jnp.where(a == 0, 0, a + 2), kzb]
                g1 = green[jnp.where(a == 0, 3, jnp.where(a == 1, 1, 5)), kzb]
                g2 = green[jnp.where(a == 2, 2, a + 4), kzb]
                half = 2 * n
                parts = [
                    g0 * spectrum[0, :, k : k + half]
                    + g1 * spectrum[1, :, k : k + half]
                    + g2 * spectrum[2, :, k : k + half]
                    for k in (0, half)
                ]
                over_y = dot3(split(jnp.concatenate(parts, axis=1)), (wh[...], wl[...]))
                both = jnp.concatenate([over_y[:, :cells], over_y[:, cells:]], axis=0)
                send[slot + 2, pl.ds(2 * a, 2)] = dot3((th[...], tl[...]), split(both)).reshape(
                    2, n, cells
                )

            exchange(slot + 2)

        arrive(turn * 4 + 2)
        arrive(turn * 4 + 3)
        scale = 1.0 / (8 * cells * cells * n)
        for a in range(3):
            total = jnp.zeros((cells, cells), F32)
            for kzb in range(2):
                rows = recv[turn * 4 + 2 + kzb, pl.ds(2 * a, 2)].reshape(2 * n, cells)
                at = slice(kzb * 2 * n, (kzb + 1) * 2 * n)
                total = total + dot3((qh[:, at], ql[:, at]), split(rows))
            image = inv_t[...] * field[a] - mask_t[...] * (total * scale)
            field[a] = image
            out[turn, a, 0] = image.T

    @pl.loop(0, 8)
    def _(slot):
        sent = send.at[slot, :, pl.ds(0, n - 1), :]
        pltpu.make_async_copy(sent, sent, send_sem.at[slot]).wait()


def per_device(n, polarization, inverse_polarizability, occupancy, green_fourier):
    cells = polarization.shape[2]
    padded = green_fourier.shape[2]
    operands = (
        polarization, inverse_polarizability, occupancy, green_fourier, *tables(n, padded)
    )
    vmem = pl.BlockSpec(memory_space=pltpu.VMEM)
    specs = [vmem] * len(operands)
    specs[3] = pl.BlockSpec(memory_space=pl.ANY)
    images = pl.pallas_call(
        functools.partial(kernel, n),
        out_shape=jax.ShapeDtypeStruct((2, *polarization.shape), F32),
        in_specs=specs,
        out_specs=vmem,
        scratch_shapes=[
            pltpu.VMEM(green_fourier.shape, F32),
            pltpu.VMEM((3, cells, cells), F32),
            pltpu.VMEM((cells, cells), F32),
            pltpu.VMEM((cells, cells), F32),
            pltpu.VMEM((8, 6, n, cells), F32),
            pltpu.VMEM((8, 6, n, cells), F32),
            pltpu.VMEM((3, padded, 2 * padded), F32),
            pltpu.SemaphoreType.DMA((8,)),
            pltpu.SemaphoreType.DMA((8,)),
            pltpu.SemaphoreType.DMA,
        ],
        compiler_params=pltpu.CompilerParams(
            has_side_effects=True, collective_id=0, vmem_limit_bytes=56 * 2**20
        ),
    )(*operands)
    return images[0], images[1]


def solution(mesh):
    return jax.shard_map(
        functools.partial(per_device, mesh.shape["slab"]),
        mesh=mesh,
        in_specs=(
            P("comp", "slab", None, None),
            P("slab", None, None),
            P("slab", None, None),
            P(None, "slab", None, None),
        ),
        out_specs=(P("comp", "slab", None, None), P("comp", "slab", None, None)),
        check_vma=False,
    )
```

profile of v0, /device:TPU:8, one launch (start us, length us, event | category | flops | bytes accessed | tf_op | source)
XLA Modules:
  0.0 101.0 jit_solution(5339337190010949165)
XLA Ops:
  0.6 98.5 %shard_map.131 = f32[2,3,1,128,128]{4,3,2,1,0:T(8,128)} custom-call(f32[3,1,128,128]{3,2,1,0:T(8,128)} %pol.1, f32[1,128,128]{2,1,0:T(8,128)} %inv.1, s32[1,16,16]{2,1,0:T(8,128)} %occ.1, f32[6,2,256,256]{3,2,1,0:T(8,128)} %green_hbm.1, bf16[512,256]{1,0:T(8,128)(2,1)} %constant.16.clone.wh, bf16[512,256]{1,0:T(8,128)(2,1)} %constant.17.clone.wl, ...), custom_call_target="tpu_custom_call" | custom-call | tf_op jit(solution)/shard_map/pallas_call | solution.py:178
  99.2 1.8 %slice_bitcast_fusion = (f32[3,1,128,128]{3,2,1,0:T(8,128)}, f32[3,1,128,128]{3,2,1,0:T(8,128)}) fusion(f32[2,3,1,128,128]{4,3,2,1,0:T(8,128)} %shard_map.131), kind=kLoop, calls=%fused_computation | loop fusion | bytes 786432
where the time goes:
time: 101 us
  Pallas kernels  98.5 us (98%)
  local copies, waits for them, and re-layouts  1.79 us (2%)
    pallas_call x1, Pallas kernels, per_device(): pl.pallas_call(functools.partial(kernel, n), out_shape=jax.ShapeDtypeStru...  98.5 us

commit v1 on v0

v1 whole, which is shorter than its diff:
```python
import functools

import jax
import jax.numpy as jnp
import numpy as np
from jax import lax
from jax.experimental import pallas as pl
from jax.experimental.pallas import tpu as pltpu
from jax.sharding import PartitionSpec as P

F32 = jnp.float32
BF16 = jnp.bfloat16
MESH = pl.DeviceIdType.MESH
ROW = 16
RING = 8
REACH = 4


def halves(table):
    table = np.asarray(table, np.float32)
    high = table.astype(BF16)
    low = (table - high.astype(np.float32)).astype(BF16)
    return high, low


def tables(n, padded):
    angle = 2.0 * np.pi / padded * (np.outer(np.arange(padded), np.arange(n)) % padded)
    cosine, sine = np.cos(angle), np.sin(angle)
    wide = np.block([[cosine, sine], [-sine, cosine]])
    planes = np.stack([part[kzb::2] for kzb in range(2) for part in (cosine, -sine)])
    return (*halves(wide), *halves(wide.T), *halves(planes))


def split(x):
    high = x.astype(BF16)
    low = (x - high.astype(F32)).astype(BF16)
    return high, low


def dot3(a, b):
    dot = functools.partial(jnp.dot, preferred_element_type=F32)
    return dot(a[0], b[0]) + dot(a[0], b[1]) + dot(a[1], b[0])


def kernel(
    n, pol, inv, occ, green_hbm, wh, wl, th, tl, ph, plo, out_0, out_1,
    green, field, inv_t, mask_t, spectrum,
    own_p, side_p, own_q, side_q,
    slab_in, part_out, part_in,
    own_s, side_s, recv, back_s, own_b, side_b,
    fwd_send, fwd_recv, back_send, back_recv, slab_send, slab_recv, part_send, part_recv, green_sem,
):
    me = lax.axis_index("slab")
    row, rank = me // ROW, lax.rem(me, ROW)
    cells = pol.shape[2]

    def at(z_row, r):
        return lax.rem(z_row + 2 * RING, RING) * ROW + r

    step_of = (1, -1)
    sides = (at(row - 1, rank), at(row + 1, rank))

    green_copy = pltpu.make_async_copy(green_hbm, green, green_sem)
    green_copy.start()

    last = (REACH - 1) * ROW
    for slot in range(4):
        for side in range(2):
            side_b[slot, side, :, last:, :] = jnp.zeros((6, ROW, cells), F32)

    barrier = pltpu.get_barrier_semaphore()
    reach = (2 * REACH - 1) * ROW

    @pl.loop(0, reach - 1)
    def _(i):
        j = i + jnp.where(i >= last + rank, 1, 0)
        pl.semaphore_signal(
            barrier,
            inc=1,
            device_id={"slab": lax.rem((row - REACH + 1 + RING) * ROW + j, n)},
            device_id_type=MESH,
        )

    blocks = occ.shape[1]
    each = cells // blocks
    spread = (
        lax.broadcasted_iota(jnp.int32, (cells, blocks), 0) // each
        == lax.broadcasted_iota(jnp.int32, (cells, blocks), 1)
    ).astype(F32)
    rows = jnp.dot(spread, occ[0].astype(F32), preferred_element_type=F32)
    mask_t[...] = lax.dot_general(
        spread, rows, (((1,), (1,)), ((), ())), preferred_element_type=F32
    )
    inv_t[...] = inv[0].T
    for c in range(3):
        field[c] = pol[c, 0].T * mask_t[...]

    for half, table in enumerate((ph, plo)):
        pick = pl.ds(pl.multiple_of(row * ROW, ROW), ROW)
        own_p[half] = table[:, pick, :]
        own_q[half] = own_p[half].astype(F32).reshape(4 * ROW, cells).T.astype(BF16)
        for side in range(2):
            for k in range(REACH):
                pick = pl.ds(pl.multiple_of(at(row + step_of[side] * k, 0), ROW), ROW)
                side_p[half, side, :, k * ROW : (k + 1) * ROW, :] = table[:, pick, :]
            side_q[half, side] = (
                side_p[half, side].astype(F32).reshape(4 * REACH * ROW, cells).T.astype(BF16)
            )

    def slab_copy(turn, c, side):
        return pltpu.make_async_remote_copy(
            src_ref=field.at[turn * 3 + c],
            dst_ref=slab_in.at[turn, side, c],
            send_sem=slab_send.at[turn, side, c],
            recv_sem=slab_recv.at[turn, side, c],
            device_id={"slab": sides[1 - side]},
            device_id_type=MESH,
        )

    def part_copy(turn, a, side):
        return pltpu.make_async_remote_copy(
            src_ref=part_out.at[turn, side, a],
            dst_ref=part_in.at[turn, side, a],
            send_sem=part_send.at[turn, side, a],
            recv_sem=part_recv.at[turn, side, a],
            device_id={"slab": sides[side]},
            device_id_type=MESH,
        )

    def place(ref, slot, lead, index, count):
        return ref.at[slot, pl.ds(lead, count), pl.ds(index, 1), :]

    def send_to(src, dst, target, send_sem, recv_sem):
        pltpu.make_async_remote_copy(
            src_ref=src, dst_ref=dst, send_sem=send_sem, recv_sem=recv_sem,
            device_id={"slab": target}, device_id_type=MESH,
        ).start()

    def messages(own, side):
        @pl.loop(1, ROW, unroll=3)
        def _(i):
            r = rank ^ i
            own(r)
            side(0, 0, r)
            side(1, 0, r)

        @pl.loop(0, ROW, unroll=2)
        def _(r):
            for k in range(1, REACH - 1):
                side(0, k, r)
                side(1, k, r)

        @pl.loop(0, ROW // 2, unroll=2)
        def _(i):
            even = 2 * i + lax.rem(rank, 2)
            side(0, REACH - 1, even)
            side(1, REACH - 1, even ^ 1)

    def forward(slot):
        sems = (fwd_send.at[slot], fwd_recv.at[slot])

        def own(r):
            send_to(
                own_s.at[slot, :, pl.ds(r, 1), :], recv.at[slot, :, pl.ds(me, 1), :],
                row * ROW + r, *sems,
            )

        def side(which, k, r):
            send_to(
                side_s.at[slot, which, :, pl.ds(k * ROW + r, 1), :],
                recv.at[slot, :, pl.ds(sides[which], 1), :],
                at(row + step_of[which] * k, r), *sems,
            )

        messages(own, side)
        recv[slot, :, pl.ds(me, 1), :] = own_s[slot, :, pl.ds(rank, 1), :]
        for which in range(2):
            recv[slot, :, pl.ds(sides[which], 1), :] = side_s[slot, which, :, pl.ds(rank, 1), :]

    count = n - 3

    def forward_wait(slot):
        landed = recv.at[slot, :, pl.ds(0, count), :]
        pltpu.make_async_copy(landed, landed, fwd_recv.at[slot]).wait()

    def backward(slot, a):
        sems = (back_send.at[slot, a], back_recv.at[slot, a])
        pair = pl.ds(2 * a, 2)

        def own(r):
            send_to(
                back_s.at[slot, pair, pl.ds(row * ROW + r, 1), :],
                own_b.at[slot, pair, pl.ds(rank, 1), :],
                row * ROW + r, *sems,
            )

        def side(which, k, r):
            collector = row - step_of[which] * k
            send_to(
                back_s.at[slot, pair, pl.ds(at(collector - step_of[which], r), 1), :],
                side_b.at[slot, which, pair, pl.ds(k * ROW + rank, 1), :],
                at(collector, r), *sems,
            )

        messages(own, side)
        own_b[slot, pair, pl.ds(rank, 1), :] = back_s[slot, pair, pl.ds(me, 1), :]
        for which in range(2):
            side_b[slot, which, pair, pl.ds(rank, 1), :] = back_s[
                slot, pair, pl.ds(sides[which], 1), :
            ]

    def backward_wait(slot, a):
        landed = back_s.at[slot, pl.ds(0, 2), pl.ds(0, count), :]
        pltpu.make_async_copy(landed, landed, back_recv.at[slot, a]).wait()

    pl.semaphore_wait(barrier, reach - 1)
    for c in range(3):
        for side in range(2):
            slab_copy(0, c, side).start()

    scale = 1.0 / (8 * cells * cells * n)

    @pl.loop(0, 2)
    def _(turn):
        for c in range(3):
            for side in range(2):
                slab_copy(turn, c, side).wait_recv()

        @pl.loop(0, 2)
        def _(kzb):
            slot = turn * 2 + kzb
            lead = pl.ds(2 * kzb, 2)
            for c in range(3):
                pair = slice(2 * c, 2 * c + 2)
                lhs = [own_p[half, lead].reshape(2 * ROW, cells) for half in range(2)]
                own_s[slot, pair] = dot3(lhs, split(field[turn * 3 + c])).reshape(2, ROW, cells)
                for side in range(2):
                    lhs = [
                        side_p[half, side, lead].reshape(2 * REACH * ROW, cells)
                        for half in range(2)
                    ]
                    side_s[slot, side, pair] = dot3(lhs, split(slab_in[turn, side, c])).reshape(
                        2, REACH * ROW, cells
                    )
            forward(slot)

        @pl.when(turn == 0)
        def _():
            green_copy.wait()

        @pl.loop(0, 2)
        def _(kzb):
            slot = turn * 2 + kzb
            forward_wait(slot)

            @pl.loop(0, 3)
            def _(c):
                rows = recv[slot, pl.ds(2 * c, 2)].reshape(2 * n, cells)
                over_x = dot3((wh[...], wl[...]), split(rows))
                both = jnp.concatenate([over_x[: 2 * n], over_x[2 * n :]], axis=1)
                spectrum[c] = dot3(split(both), (th[...], tl[...]))

            @pl.loop(0, 3)
            def _(a):
                g0 = green[jnp.where(a == 0, 0, a + 2), kzb]
                g1 = green[jnp.where(a == 0, 3, jnp.where(a == 1, 1, 5)), kzb]
                g2 = green[jnp.where(a == 2, 2, a + 4), kzb]
                half = 2 * n
                parts = [
                    g0 * spectrum[0, :, k : k + half]
                    + g1 * spectrum[1, :, k : k + half]
                    + g2 * spectrum[2, :, k : k + half]
                    for k in (0, half)
                ]
                over_y = dot3(split(jnp.concatenate(parts, axis=1)), (wh[...], wl[...]))
                both = jnp.concatenate([over_y[:, :cells], over_y[:, cells:]], axis=0)
                back_s[slot, pl.ds(2 * a, 2)] = dot3((th[...], tl[...]), split(both)).reshape(
                    2, n, cells
                )
                backward(slot, a)

        def collect(a):
            for kzb in range(2):
                backward_wait(turn * 2 + kzb, a)
            for side in range(2):
                rows = jnp.concatenate(
                    [
                        side_b[turn * 2 + kzb, side, 2 * a : 2 * a + 2].reshape(-1, cells)
                        for kzb in range(2)
                    ]
                )
                part_out[turn, side, a] = dot3([side_q[half, side] for half in range(2)], split(rows))
                part_copy(turn, a, side).start()

        def finish(a):
            rows = jnp.concatenate(
                [
                    own_b[turn * 2 + kzb, 2 * a : 2 * a + 2].reshape(-1, cells)
                    for kzb in range(2)
                ]
            )
            total = dot3([own_q[half] for half in range(2)], split(rows))
            for side in range(2):
                part_copy(turn, a, side).wait_recv()
            total = total + part_in[turn, 0, a] + part_in[turn, 1, a]
            image = inv_t[...] * field[turn * 3 + a] - mask_t[...] * (total * scale)

            @pl.when(turn == 0)
            def _():
                field[3 + a] = image * mask_t[...]
                for side in range(2):
                    slab_copy(1, a, side).start()
                out_0[a, 0] = image.T

            @pl.when(turn == 1)
            def _():
                out_1[a, 0] = image.T

        collect(0)
        collect(1)
        finish(0)
        collect(2)
        finish(1)
        finish(2)

    @pl.loop(0, 4)
    def _(slot):
        sent = recv.at[slot, :, pl.ds(0, count), :]
        pltpu.make_async_copy(sent, sent, fwd_send.at[slot]).wait()
        for a in range(3):
            sent = back_s.at[slot, pl.ds(0, 2), pl.ds(0, count), :]
            pltpu.make_async_copy(sent, sent, back_send.at[slot, a]).wait()

    @pl.loop(0, 2)
    def _(turn):
        for c in range(3):
            for side in range(2):
                slab_copy(turn, c, side).wait_send()
                part_copy(turn, c, side).wait_send()


def per_device(n, polarization, inverse_polarizability, occupancy, green_fourier):
    cells = polarization.shape[2]
    padded = green_fourier.shape[2]
    operands = (
        polarization, inverse_polarizability, occupancy, green_fourier, *tables(n, padded)
    )
    vmem = pl.BlockSpec(memory_space=pltpu.VMEM)
    specs = [vmem] * len(operands)
    specs[3] = pl.BlockSpec(memory_space=pl.ANY)
    span = REACH * ROW
    image = jax.ShapeDtypeStruct(polarization.shape, F32)
    dma = pltpu.SemaphoreType.DMA
    return pl.pallas_call(
        functools.partial(kernel, n),
        out_shape=(image, image),
        in_specs=specs,
        out_specs=(vmem, vmem),
        scratch_shapes=[
            pltpu.VMEM(green_fourier.shape, F32),
            pltpu.VMEM((6, cells, cells), F32),
            pltpu.VMEM((cells, cells), F32),
            pltpu.VMEM((cells, cells), F32),
            pltpu.VMEM((3, padded, 2 * padded), F32),
            pltpu.VMEM((2, 4, ROW, cells), BF16),
            pltpu.VMEM((2, 2, 4, span, cells), BF16),
            pltpu.VMEM((2, cells, 4 * ROW), BF16),
            pltpu.VMEM((2, 2, cells, 4 * span), BF16),
            pltpu.VMEM((2, 2, 3, cells, cells), F32),
            pltpu.VMEM((2, 2, 3, cells, cells), F32),
            pltpu.VMEM((2, 2, 3, cells, cells), F32),
            pltpu.VMEM((4, 6, ROW, cells), F32),
            pltpu.VMEM((4, 2, 6, span, cells), F32),
            pltpu.VMEM((4, 6, n, cells), F32),
            pltpu.VMEM((4, 6, n, cells), F32),
            pltpu.VMEM((4, 6, ROW, cells), F32),
            pltpu.VMEM((4, 2, 6, span, cells), F32),
            dma((4,)), dma((4,)), dma((4, 3)), dma((4, 3)),
            dma((2, 2, 3)), dma((2, 2, 3)), dma((2, 2, 3)), dma((2, 2, 3)), dma,
        ],
        compiler_params=pltpu.CompilerParams(
            has_side_effects=True, collective_id=0, vmem_limit_bytes=56 * 2**20
        ),
    )(*operands)


def solution(mesh):
    return jax.shard_map(
        functools.partial(per_device, mesh.shape["slab"]),
        mesh=mesh,
        in_specs=(
            P("comp", "slab", None, None),
            P("slab", None, None),
            P("slab", None, None),
            P(None, "slab", None, None),
        ),
        out_specs=(P("comp", "slab", None, None), P("comp", "slab", None, None)),
        check_vma=False,
    )
```

time: 101 us -> 113 us (1.12)
  Pallas kernels: 98.5 us -> 109 us
  local copies, waits for them, and re-layouts: 1.79 us -> 3.23 us
    pallas_call x1, Pallas kernels: 98.5 us -> 109 us  [per_device(): pl.pallas_call(functools.partial(kernel, n), out_shape=(image, image), in...]
    unnamed x1 -> x2, local copies, waits for them, and re-layouts: 1.79 us -> 3.23 us
where the time goes in v1:
time: 113 us; the launch traced here: 112 us
  Pallas kernels  109 us (96%)
  local copies, waits for them, and re-layouts  3.23 us (3%)
    pallas_call x1, Pallas kernels, per_device(): pl.pallas_call(functools.partial(kernel, n), out_shape=(image, image), in...  109 us
    unnamed x2, local copies, waits for them, and re-layouts  3.23 us

profile of v1, /device:TPU:8, one launch (start us, length us, event | category | flops | bytes accessed | tf_op | source)
XLA Modules:
  0.0 112.4 jit_solution(4259170444531373177)
XLA Ops:
  0.6 108.5 %shard_map.113 = (f32[3,1,128,128]{3,2,1,0:T(8,128)}, f32[3,1,128,128]{3,2,1,0:T(8,128)}) custom-call(f32[3,1,128,128]{3,2,1,0:T(8,128)} %pol.1, f32[1,128,128]{2,1,0:T(8,128)} %inv.1, s32[1,16,16]{2,1,0:T(8,128)} %occ.1, f32[6,2,256,256]{3,2,1,0:T(8,128)} %green_hbm.1, bf16[512,256]{1,0:T(8,128)(2,1)} %constant.12.clone.wh, ...), custom_call_target="tpu_custom_call" | custom-call | tf_op jit(solution)/shard_map/pallas_call | solution.py:354
  109.2 1.6 %copy.14 = f32[3,1,128,128]{3,2,1,0:T(8,128)} copy(f32[3,1,128,128]{3,2,1,0:T(8,128)} %get-tuple-element.4) | data formatting | bytes 393216
  110.8 1.6 %copy.15 = f32[3,1,128,128]{3,2,1,0:T(8,128)} copy(f32[3,1,128,128]{3,2,1,0:T(8,128)} %get-tuple-element.5) | data formatting | bytes 393216

commit v2 on v1

--- a/solution.py
+++ b/solution.py
@@ -43,12 +43,14 @@
 
 
 def kernel(
-    n, pol, inv, occ, green_hbm, wh, wl, th, tl, ph, plo, out_0, out_1,
-    green, field, inv_t, mask_t, spectrum,
+    n, pol_hbm, inv_hbm, occ_hbm, green_hbm, wh_hbm, wl_hbm, th_hbm, tl_hbm, ph_hbm, pl_hbm,
+    out_0, out_1,
+    pol, inv, occ, green, wh, wl, th, tl, ph, plo, over_x, images,
+    field, inv_t, mask_t, spectrum,
     own_p, side_p, own_q, side_q,
     slab_in, part_out, part_in,
     own_s, side_s, recv, back_s, own_b, side_b,
-    fwd_send, fwd_recv, back_send, back_recv, slab_send, slab_recv, part_send, part_recv, green_sem,
+    fwd_send, fwd_recv, back_send, back_recv, slab_send, slab_recv, part_send, part_recv, first_sem, later_sem, out_sem,
 ):
     me = lax.axis_index("slab")
     row, rank = me // ROW, lax.rem(me, ROW)
@@ -59,9 +61,6 @@
 
     step_of = (1, -1)
     sides = (at(row - 1, rank), at(row + 1, rank))
-
-    green_copy = pltpu.make_async_copy(green_hbm, green, green_sem)
-    green_copy.start()
 
     last = (REACH - 1) * ROW
     for slot in range(4):
@@ -80,6 +79,23 @@
             device_id={"slab": lax.rem((row - REACH + 1 + RING) * ROW + j, n)},
             device_id_type=MESH,
         )
+
+    first = [
+        pltpu.make_async_copy(src, dst, first_sem.at[i])
+        for i, (src, dst) in enumerate(
+            ((occ_hbm, occ), (pol_hbm, pol), (ph_hbm, ph), (pl_hbm, plo), (inv_hbm, inv))
+        )
+    ]
+    later = [
+        pltpu.make_async_copy(src, dst, later_sem.at[i])
+        for i, (src, dst) in enumerate(
+            ((wh_hbm, wh), (wl_hbm, wl), (th_hbm, th), (tl_hbm, tl), (green_hbm, green))
+        )
+    ]
+    for copy in (*first, *later):
+        copy.start()
+    for copy in first:
+        copy.wait()
 
     blocks = occ.shape[1]
     each = cells // blocks
@@ -127,8 +143,9 @@
             device_id_type=MESH,
         )
 
-    def place(ref, slot, lead, index, count):
-        return ref.at[slot, pl.ds(lead, count), pl.ds(index, 1), :]
+    def out_copy(turn, a):
+        out = (out_0, out_1)[turn]
+        return pltpu.make_async_copy(images.at[turn, a], out.at[a, 0], out_sem.at[turn, a])
 
     def send_to(src, dst, target, send_sem, recv_sem):
         pltpu.make_async_remote_copy(
@@ -183,35 +200,32 @@
         landed = recv.at[slot, :, pl.ds(0, count), :]
         pltpu.make_async_copy(landed, landed, fwd_recv.at[slot]).wait()
 
-    def backward(slot, a):
-        sems = (back_send.at[slot, a], back_recv.at[slot, a])
-        pair = pl.ds(2 * a, 2)
+    def backward(slot):
+        sems = (back_send.at[slot], back_recv.at[slot])
 
         def own(r):
             send_to(
-                back_s.at[slot, pair, pl.ds(row * ROW + r, 1), :],
-                own_b.at[slot, pair, pl.ds(rank, 1), :],
+                back_s.at[slot, :, pl.ds(row * ROW + r, 1), :],
+                own_b.at[slot, :, pl.ds(rank, 1), :],
                 row * ROW + r, *sems,
             )
 
         def side(which, k, r):
             collector = row - step_of[which] * k
             send_to(
-                back_s.at[slot, pair, pl.ds(at(collector - step_of[which], r), 1), :],
-                side_b.at[slot, which, pair, pl.ds(k * ROW + rank, 1), :],
+                back_s.at[slot, :, pl.ds(at(collector - step_of[which], r), 1), :],
+                side_b.at[slot, which, :, pl.ds(k * ROW + rank, 1), :],
                 at(collector, r), *sems,
             )
 
         messages(own, side)
-        own_b[slot, pair, pl.ds(rank, 1), :] = back_s[slot, pair, pl.ds(me, 1), :]
+        own_b[slot, :, pl.ds(rank, 1), :] = back_s[slot, :, pl.ds(me, 1), :]
         for which in range(2):
-            side_b[slot, which, pair, pl.ds(rank, 1), :] = back_s[
-                slot, pair, pl.ds(sides[which], 1), :
-            ]
-
-    def backward_wait(slot, a):
-        landed = back_s.at[slot, pl.ds(0, 2), pl.ds(0, count), :]
-        pltpu.make_async_copy(landed, landed, back_recv.at[slot, a]).wait()
+            side_b[slot, which, :, pl.ds(rank, 1), :] = back_s[slot, :, pl.ds(sides[which], 1), :]
+
+    def backward_wait(slot):
+        landed = back_s.at[slot, :, pl.ds(0, count), :]
+        pltpu.make_async_copy(landed, landed, back_recv.at[slot]).wait()
 
     pl.semaphore_wait(barrier, reach - 1)
     for c in range(3):
@@ -220,8 +234,7 @@
 
     scale = 1.0 / (8 * cells * cells * n)
 
-    @pl.loop(0, 2)
-    def _(turn):
+    for turn in range(2):
         for c in range(3):
             for side in range(2):
                 slab_copy(turn, c, side).wait_recv()
@@ -244,96 +257,80 @@
                     )
             forward(slot)
 
-        @pl.when(turn == 0)
-        def _():
-            green_copy.wait()
+        if turn == 0:
+            for copy in later:
+                copy.wait()
 
         @pl.loop(0, 2)
         def _(kzb):
             slot = turn * 2 + kzb
             forward_wait(slot)
-
-            @pl.loop(0, 3)
-            def _(c):
-                rows = recv[slot, pl.ds(2 * c, 2)].reshape(2 * n, cells)
-                over_x = dot3((wh[...], wl[...]), split(rows))
-                both = jnp.concatenate([over_x[: 2 * n], over_x[2 * n :]], axis=1)
-                spectrum[c] = dot3(split(both), (th[...], tl[...]))
-
-            @pl.loop(0, 3)
-            def _(a):
-                g0 = green[jnp.where(a == 0, 0, a + 2), kzb]
-                g1 = green[jnp.where(a == 0, 3, jnp.where(a == 1, 1, 5)), kzb]
-                g2 = green[jnp.where(a == 2, 2, a + 4), kzb]
-                half = 2 * n
+            half = 2 * n
+            rows = split(
+                jnp.concatenate(
+                    [recv[slot, 2 * c : 2 * c + 2].reshape(half, cells) for c in range(3)], axis=1
+                )
+            )
+            for part in range(2):
+                at_rows = slice(part * half, (part + 1) * half)
+                product = dot3((wh[at_rows], wl[at_rows]), rows)
+                for c in range(3):
+                    over_x[c, :, part * cells : (part + 1) * cells] = product[
+                        :, c * cells : (c + 1) * cells
+                    ]
+            for c in range(3):
+                spectrum[c] = dot3(split(over_x[c]), (th[...], tl[...]))
+            for a, combo in enumerate(((0, 3, 4), (3, 1, 5), (4, 5, 2))):
                 parts = [
-                    g0 * spectrum[0, :, k : k + half]
-                    + g1 * spectrum[1, :, k : k + half]
-                    + g2 * spectrum[2, :, k : k + half]
+                    green[combo[0], kzb] * spectrum[0, :, k : k + half]
+                    + green[combo[1], kzb] * spectrum[1, :, k : k + half]
+                    + green[combo[2], kzb] * spectrum[2, :, k : k + half]
                     for k in (0, half)
                 ]
                 over_y = dot3(split(jnp.concatenate(parts, axis=1)), (wh[...], wl[...]))
                 both = jnp.concatenate([over_y[:, :cells], over_y[:, cells:]], axis=0)
-                back_s[slot, pl.ds(2 * a, 2)] = dot3((th[...], tl[...]), split(both)).reshape(
+                back_s[slot, 2 * a : 2 * a + 2] = dot3((th[...], tl[...]), split(both)).reshape(
                     2, n, cells
                 )
-                backward(slot, a)
-
-        def collect(a):
-            for kzb in range(2):
-                backward_wait(turn * 2 + kzb, a)
+            backward(slot)
+
+        slots = (turn * 2, turn * 2 + 1)
+        for slot in slots:
+            backward_wait(slot)
+        for a in range(3):
             for side in range(2):
                 rows = jnp.concatenate(
-                    [
-                        side_b[turn * 2 + kzb, side, 2 * a : 2 * a + 2].reshape(-1, cells)
-                        for kzb in range(2)
-                    ]
+                    [side_b[slot, side, 2 * a : 2 * a + 2].reshape(-1, cells) for slot in slots]
                 )
-                part_out[turn, side, a] = dot3([side_q[half, side] for half in range(2)], split(rows))
+                part_out[turn, side, a] = dot3((side_q[0, side], side_q[1, side]), split(rows))
                 part_copy(turn, a, side).start()
-
-        def finish(a):
+        totals = []
+        for a in range(3):
             rows = jnp.concatenate(
-                [
-                    own_b[turn * 2 + kzb, 2 * a : 2 * a + 2].reshape(-1, cells)
-                    for kzb in range(2)
-                ]
-            )
-            total = dot3([own_q[half] for half in range(2)], split(rows))
+                [own_b[slot, 2 * a : 2 * a + 2].reshape(-1, cells) for slot in slots]
+            )
+            totals.append(dot3((own_q[0], own_q[1]), split(rows)))
+        for a in range(3):
             for side in range(2):
                 part_copy(turn, a, side).wait_recv()
-            total = total + part_in[turn, 0, a] + part_in[turn, 1, a]
+            total = totals[a] + part_in[turn, 0, a] + part_in[turn, 1, a]
             image = inv_t[...] * field[turn * 3 + a] - mask_t[...] * (total * scale)
-
-            @pl.when(turn == 0)
-            def _():
+            if turn == 0:
                 field[3 + a] = image * mask_t[...]
                 for side in range(2):
                     slab_copy(1, a, side).start()
-                out_0[a, 0] = image.T
-
-            @pl.when(turn == 1)
-            def _():
-                out_1[a, 0] = image.T
-
-        collect(0)
-        collect(1)
-        finish(0)
-        collect(2)
-        finish(1)
-        finish(2)
+            images[turn, a] = image.T
+            out_copy(turn, a).start()
 
     @pl.loop(0, 4)
     def _(slot):
         sent = recv.at[slot, :, pl.ds(0, count), :]
         pltpu.make_async_copy(sent, sent, fwd_send.at[slot]).wait()
-        for a in range(3):
-            sent = back_s.at[slot, pl.ds(0, 2), pl.ds(0, count), :]
-            pltpu.make_async_copy(sent, sent, back_send.at[slot, a]).wait()
-
-    @pl.loop(0, 2)
-    def _(turn):
+        pltpu.make_async_copy(sent, sent, back_send.at[slot]).wait()
+
+    for turn in range(2):
         for c in range(3):
+            out_copy(turn, c).wait()
             for side in range(2):
                 slab_copy(turn, c, side).wait_send()
                 part_copy(turn, c, side).wait_send()
@@ -345,19 +342,19 @@
     operands = (
         polarization, inverse_polarizability, occupancy, green_fourier, *tables(n, padded)
     )
-    vmem = pl.BlockSpec(memory_space=pltpu.VMEM)
-    specs = [vmem] * len(operands)
-    specs[3] = pl.BlockSpec(memory_space=pl.ANY)
     span = REACH * ROW
     image = jax.ShapeDtypeStruct(polarization.shape, F32)
     dma = pltpu.SemaphoreType.DMA
+    anywhere = pl.BlockSpec(memory_space=pl.ANY)
     return pl.pallas_call(
         functools.partial(kernel, n),
         out_shape=(image, image),
-        in_specs=specs,
-        out_specs=(vmem, vmem),
+        in_specs=[anywhere] * len(operands),
+        out_specs=(anywhere, anywhere),
         scratch_shapes=[
-            pltpu.VMEM(green_fourier.shape, F32),
+            *(pltpu.VMEM(x.shape, x.dtype) for x in operands),
+            pltpu.VMEM((3, padded, padded), F32),
+            pltpu.VMEM((2, 3, cells, cells), F32),
             pltpu.VMEM((6, cells, cells), F32),
             pltpu.VMEM((cells, cells), F32),
             pltpu.VMEM((cells, cells), F32),
@@ -375,8 +372,8 @@
             pltpu.VMEM((4, 6, n, cells), F32),
             pltpu.VMEM((4, 6, ROW, cells), F32),
             pltpu.VMEM((4, 2, 6, span, cells), F32),
-            dma((4,)), dma((4,)), dma((4, 3)), dma((4, 3)),
-            dma((2, 2, 3)), dma((2, 2, 3)), dma((2, 2, 3)), dma((2, 2, 3)), dma,
+            dma((4,)), dma((4,)), dma((4,)), dma((4,)),
+            dma((2, 2, 3)), dma((2, 2, 3)), dma((2, 2, 3)), dma((2, 2, 3)), dma((5,)), dma((5,)), dma((2, 3)),
         ],
         compiler_params=pltpu.CompilerParams(
             has_side_effects=True, collective_id=0, vmem_limit_bytes=56 * 2**20

time: 113 us -> 98.5 us (0.87)
  Pallas kernels: 109 us -> 94.3 us
    pallas_call x1, Pallas kernels: 109 us -> 94.3 us  [per_device(): pl.pallas_call(functools.partial(kernel, n), out_shape=(image, image), in...]
where the time goes in v2:
time: 98.5 us; the launch traced here: 98.2 us
  Pallas kernels  94.3 us (96%)
  local copies, waits for them, and re-layouts  3.23 us (3%)
    pallas_call x1, Pallas kernels, per_device(): pl.pallas_call(functools.partial(kernel, n), out_shape=(image, image), in...  94.3 us
    unnamed x2, local copies, waits for them, and re-layouts  3.23 us

profile of v2, /device:TPU:8, one launch (start us, length us, event | category | flops | bytes accessed | tf_op | source)
XLA Modules:
  0.0 98.2 jit_solution(16314789370604393598)
XLA Ops:
  0.6 94.3 %shard_map.113 = (f32[3,1,128,128]{3,2,1,0:T(8,128)}, f32[3,1,128,128]{3,2,1,0:T(8,128)}) custom-call(f32[3,1,128,128]{3,2,1,0:T(8,128)} %pol_hbm.1, f32[1,128,128]{2,1,0:T(8,128)} %inv_hbm.1, s32[1,16,16]{2,1,0:T(8,128)} %occ_hbm.1, f32[6,2,256,256]{3,2,1,0:T(8,128)} %green_hbm.1, bf16[512,256]{1,0:T(8,128)(2,1)} %constant.12.clone.wh_hbm, ...), custom_call_target="tpu_custom_call" | custom-call | tf_op jit(solution)/shard_map/pallas_call | solution.py:349
  94.9 1.6 %copy.14 = f32[3,1,128,128]{3,2,1,0:T(8,128)} copy(f32[3,1,128,128]{3,2,1,0:T(8,128)} %get-tuple-element.4) | data formatting | bytes 393216
  96.6 1.6 %copy.15 = f32[3,1,128,128]{3,2,1,0:T(8,128)} copy(f32[3,1,128,128]{3,2,1,0:T(8,128)} %get-tuple-element.5) | data formatting | bytes 393216

commit v3 on v2

--- a/solution.py
+++ b/solution.py
@@ -173,59 +173,62 @@
             side(0, REACH - 1, even)
             side(1, REACH - 1, even ^ 1)
 
-    def forward(slot):
-        sems = (fwd_send.at[slot], fwd_recv.at[slot])
+    def forward(slot, low, width, sem):
+        sems = (fwd_send.at[sem], fwd_recv.at[sem])
+        span = pl.ds(low, width)
 
         def own(r):
             send_to(
-                own_s.at[slot, :, pl.ds(r, 1), :], recv.at[slot, :, pl.ds(me, 1), :],
+                own_s.at[slot, span, pl.ds(r, 1), :], recv.at[slot, span, pl.ds(me, 1), :],
                 row * ROW + r, *sems,
             )
 
         def side(which, k, r):
             send_to(
-                side_s.at[slot, which, :, pl.ds(k * ROW + r, 1), :],
-                recv.at[slot, :, pl.ds(sides[which], 1), :],
+                side_s.at[slot, which, span, pl.ds(k * ROW + r, 1), :],
+                recv.at[slot, span, pl.ds(sides[which], 1), :],
                 at(row + step_of[which] * k, r), *sems,
             )
 
         messages(own, side)
-        recv[slot, :, pl.ds(me, 1), :] = own_s[slot, :, pl.ds(rank, 1), :]
+        recv[slot, span, pl.ds(me, 1), :] = own_s[slot, span, pl.ds(rank, 1), :]
         for which in range(2):
-            recv[slot, :, pl.ds(sides[which], 1), :] = side_s[slot, which, :, pl.ds(rank, 1), :]
-
-    count = n - 3
-
-    def forward_wait(slot):
-        landed = recv.at[slot, :, pl.ds(0, count), :]
-        pltpu.make_async_copy(landed, landed, fwd_recv.at[slot]).wait()
-
-    def backward(slot):
-        sems = (back_send.at[slot], back_recv.at[slot])
+            recv[slot, span, pl.ds(sides[which], 1), :] = side_s[
+                slot, which, span, pl.ds(rank, 1), :
+            ]
+
+    def backward(slot, low, width, sem):
+        sems = (back_send.at[sem], back_recv.at[sem])
+        span = pl.ds(low, width)
 
         def own(r):
             send_to(
-                back_s.at[slot, :, pl.ds(row * ROW + r, 1), :],
-                own_b.at[slot, :, pl.ds(rank, 1), :],
+                back_s.at[slot, span, pl.ds(row * ROW + r, 1), :],
+                own_b.at[slot, span, pl.ds(rank, 1), :],
                 row * ROW + r, *sems,
             )
 
         def side(which, k, r):
             collector = row - step_of[which] * k
             send_to(
-                back_s.at[slot, :, pl.ds(at(collector - step_of[which], r), 1), :],
-                side_b.at[slot, which, :, pl.ds(k * ROW + rank, 1), :],
+                back_s.at[slot, span, pl.ds(at(collector - step_of[which], r), 1), :],
+                side_b.at[slot, which, span, pl.ds(k * ROW + rank, 1), :],
                 at(collector, r), *sems,
             )
 
         messages(own, side)
-        own_b[slot, :, pl.ds(rank, 1), :] = back_s[slot, :, pl.ds(me, 1), :]
+        own_b[slot, span, pl.ds(rank, 1), :] = back_s[slot, span, pl.ds(me, 1), :]
         for which in range(2):
-            side_b[slot, which, :, pl.ds(rank, 1), :] = back_s[slot, :, pl.ds(sides[which], 1), :]
-
-    def backward_wait(slot):
-        landed = back_s.at[slot, :, pl.ds(0, count), :]
-        pltpu.make_async_copy(landed, landed, back_recv.at[slot]).wait()
+            side_b[slot, which, span, pl.ds(rank, 1), :] = back_s[
+                slot, span, pl.ds(sides[which], 1), :
+            ]
+
+    def wait_for(ref, width, sem):
+        bytes_of = ref.at[0, pl.ds(0, width), pl.ds(0, n - 3), :]
+        pltpu.make_async_copy(bytes_of, bytes_of, sem).wait()
+
+    fwd_plan = ((0, 0, 2), (0, 2, 2), (0, 4, 2), (1, 0, 6))
+    back_plan = ((0, 0, 6), (1, 0, 2), (1, 2, 2), (1, 4, 2))
 
     pl.semaphore_wait(barrier, reach - 1)
     for c in range(3):
@@ -234,38 +237,33 @@
 
     scale = 1.0 / (8 * cells * cells * n)
 
+    half = 2 * n
     for turn in range(2):
+        slots = (2 * turn, 2 * turn + 1)
         for c in range(3):
             for side in range(2):
                 slab_copy(turn, c, side).wait_recv()
-
-        @pl.loop(0, 2)
-        def _(kzb):
-            slot = turn * 2 + kzb
-            lead = pl.ds(2 * kzb, 2)
-            for c in range(3):
-                pair = slice(2 * c, 2 * c + 2)
-                lhs = [own_p[half, lead].reshape(2 * ROW, cells) for half in range(2)]
-                own_s[slot, pair] = dot3(lhs, split(field[turn * 3 + c])).reshape(2, ROW, cells)
-                for side in range(2):
-                    lhs = [
-                        side_p[half, side, lead].reshape(2 * REACH * ROW, cells)
-                        for half in range(2)
-                    ]
-                    side_s[slot, side, pair] = dot3(lhs, split(slab_in[turn, side, c])).reshape(
-                        2, REACH * ROW, cells
-                    )
-            forward(slot)
+            pair = slice(2 * c, 2 * c + 2)
+            lhs = [own_p[part].reshape(4 * ROW, cells) for part in range(2)]
+            product = dot3(lhs, split(field[turn * 3 + c])).reshape(4, ROW, cells)
+            for kzb, slot in enumerate(slots):
+                own_s[slot, pair] = product[2 * kzb : 2 * kzb + 2]
+            for side in range(2):
+                lhs = [side_p[part, side].reshape(4 * REACH * ROW, cells) for part in range(2)]
+                product = dot3(lhs, split(slab_in[turn, side, c])).reshape(4, REACH * ROW, cells)
+                for kzb, slot in enumerate(slots):
+                    side_s[slot, side, pair] = product[2 * kzb : 2 * kzb + 2]
+            forward(slots[0], 2 * c, 2, 4 * turn + c)
+        forward(slots[1], 0, 6, 4 * turn + 3)
 
         if turn == 0:
             for copy in later:
                 copy.wait()
 
-        @pl.loop(0, 2)
-        def _(kzb):
-            slot = turn * 2 + kzb
-            forward_wait(slot)
-            half = 2 * n
+        for kzb, slot in enumerate(slots):
+            for sem, (plane, low, width) in enumerate(fwd_plan):
+                if plane == kzb:
+                    wait_for(recv, width, fwd_recv.at[4 * turn + sem])
             rows = split(
                 jnp.concatenate(
                     [recv[slot, 2 * c : 2 * c + 2].reshape(half, cells) for c in range(3)], axis=1
@@ -292,20 +290,21 @@
                 back_s[slot, 2 * a : 2 * a + 2] = dot3((th[...], tl[...]), split(both)).reshape(
                     2, n, cells
                 )
-            backward(slot)
-
-        slots = (turn * 2, turn * 2 + 1)
-        for slot in slots:
-            backward_wait(slot)
+                if kzb == 1:
+                    backward(slot, 2 * a, 2, 4 * turn + 1 + a)
+            if kzb == 0:
+                backward(slot, 0, 6, 4 * turn)
+
+        wait_for(recv, 6, back_recv.at[4 * turn])
+        totals = []
         for a in range(3):
+            wait_for(recv, 2, back_recv.at[4 * turn + 1 + a])
             for side in range(2):
                 rows = jnp.concatenate(
                     [side_b[slot, side, 2 * a : 2 * a + 2].reshape(-1, cells) for slot in slots]
                 )
                 part_out[turn, side, a] = dot3((side_q[0, side], side_q[1, side]), split(rows))
                 part_copy(turn, a, side).start()
-        totals = []
-        for a in range(3):
             rows = jnp.concatenate(
                 [own_b[slot, 2 * a : 2 * a + 2].reshape(-1, cells) for slot in slots]
             )
@@ -322,11 +321,10 @@
             images[turn, a] = image.T
             out_copy(turn, a).start()
 
-    @pl.loop(0, 4)
-    def _(slot):
-        sent = recv.at[slot, :, pl.ds(0, count), :]
-        pltpu.make_async_copy(sent, sent, fwd_send.at[slot]).wait()
-        pltpu.make_async_copy(sent, sent, back_send.at[slot]).wait()
+    for turn in range(2):
+        for plan, sems in ((fwd_plan, fwd_send), (back_plan, back_send)):
+            for sem, (_, _, width) in enumerate(plan):
+                wait_for(recv, width, sems.at[4 * turn + sem])
 
     for turn in range(2):
         for c in range(3):
@@ -372,7 +370,7 @@
             pltpu.VMEM((4, 6, n, cells), F32),
             pltpu.VMEM((4, 6, ROW, cells), F32),
             pltpu.VMEM((4, 2, 6, span, cells), F32),
-            dma((4,)), dma((4,)), dma((4,)), dma((4,)),
+            dma((8,)), dma((8,)), dma((8,)), dma((8,)),
             dma((2, 2, 3)), dma((2, 2, 3)), dma((2, 2, 3)), dma((2, 2, 3)), dma((5,)), dma((5,)), dma((2, 3)),
         ],
         compiler_params=pltpu.CompilerParams(

time: 98.5 us -> 93.3 us (0.947)
  Pallas kernels: 94.3 us -> 89.3 us
    pallas_call x1, Pallas kernels: 94.3 us -> 89.3 us  [per_device(): pl.pallas_call(functools.partial(kernel, n), out_shape=(image, image), in...]
where the time goes in v3:
time: 93.3 us; the launch traced here: 93.2 us
  Pallas kernels  89.3 us (96%)
  local copies, waits for them, and re-layouts  3.23 us (3%)
    pallas_call x1, Pallas kernels, per_device(): pl.pallas_call(functools.partial(kernel, n), out_shape=(image, image), in...  89.3 us
    unnamed x2, local copies, waits for them, and re-layouts  3.23 us

profile of v3, /device:TPU:8, one launch (start us, length us, event | category | flops | bytes accessed | tf_op | source)
XLA Modules:
  0.0 93.2 jit_solution(637356283856273635)
XLA Ops:
  0.6 89.3 %shard_map.113 = (f32[3,1,128,128]{3,2,1,0:T(8,128)}, f32[3,1,128,128]{3,2,1,0:T(8,128)}) custom-call(f32[3,1,128,128]{3,2,1,0:T(8,128)} %pol_hbm.1, f32[1,128,128]{2,1,0:T(8,128)} %inv_hbm.1, s32[1,16,16]{2,1,0:T(8,128)} %occ_hbm.1, f32[6,2,256,256]{3,2,1,0:T(8,128)} %green_hbm.1, bf16[512,256]{1,0:T(8,128)(2,1)} %constant.12.clone.wh_hbm, ...), custom_call_target="tpu_custom_call" | custom-call | tf_op jit(solution)/shard_map/pallas_call | solution.py:347
  90.0 1.6 %copy.14 = f32[3,1,128,128]{3,2,1,0:T(8,128)} copy(f32[3,1,128,128]{3,2,1,0:T(8,128)} %get-tuple-element.4) | data formatting | bytes 393216
  91.6 1.6 %copy.15 = f32[3,1,128,128]{3,2,1,0:T(8,128)} copy(f32[3,1,128,128]{3,2,1,0:T(8,128)} %get-tuple-element.5) | data formatting | bytes 393216

commit v4 on v3

--- a/solution.py
+++ b/solution.py
@@ -68,17 +68,20 @@
             side_b[slot, side, :, last:, :] = jnp.zeros((6, ROW, cells), F32)
 
     barrier = pltpu.get_barrier_semaphore()
-    reach = (2 * REACH - 1) * ROW
-
-    @pl.loop(0, reach - 1)
+
+    def greet(target):
+        pl.semaphore_signal(barrier, inc=1, device_id={"slab": target}, device_id_type=MESH)
+
+    for k in range(REACH - 1, 0, -1):
+
+        @pl.loop(0, ROW, unroll=4)
+        def _(r):
+            greet(at(row + k, r))
+            greet(at(row - k, r))
+
+    @pl.loop(1, ROW, unroll=3)
     def _(i):
-        j = i + jnp.where(i >= last + rank, 1, 0)
-        pl.semaphore_signal(
-            barrier,
-            inc=1,
-            device_id={"slab": lax.rem((row - REACH + 1 + RING) * ROW + j, n)},
-            device_id_type=MESH,
-        )
+        greet(row * ROW + (rank ^ i))
 
     first = [
         pltpu.make_async_copy(src, dst, first_sem.at[i])
@@ -154,24 +157,25 @@
         ).start()
 
     def messages(own, side):
-        @pl.loop(1, ROW, unroll=3)
-        def _(i):
-            r = rank ^ i
-            own(r)
-            side(0, 0, r)
-            side(1, 0, r)
-
-        @pl.loop(0, ROW, unroll=2)
-        def _(r):
-            for k in range(1, REACH - 1):
-                side(0, k, r)
-                side(1, k, r)
-
         @pl.loop(0, ROW // 2, unroll=2)
         def _(i):
             even = 2 * i + lax.rem(rank, 2)
             side(0, REACH - 1, even)
             side(1, REACH - 1, even ^ 1)
+
+        for k in range(REACH - 2, 0, -1):
+
+            @pl.loop(0, ROW, unroll=4)
+            def _(r):
+                side(0, k, r)
+                side(1, k, r)
+
+        @pl.loop(1, ROW, unroll=3)
+        def _(i):
+            r = rank ^ i
+            side(0, 0, r)
+            side(1, 0, r)
+            own(r)
 
     def forward(slot, low, width, sem):
         sems = (fwd_send.at[sem], fwd_recv.at[sem])
@@ -230,7 +234,7 @@
     fwd_plan = ((0, 0, 2), (0, 2, 2), (0, 4, 2), (1, 0, 6))
     back_plan = ((0, 0, 6), (1, 0, 2), (1, 2, 2), (1, 4, 2))
 
-    pl.semaphore_wait(barrier, reach - 1)
+    pl.semaphore_wait(barrier, (2 * REACH - 1) * ROW - 1)
     for c in range(3):
         for side in range(2):
             slab_copy(0, c, side).start()

time: 93.3 us -> 88.5 us (0.949)
  Pallas kernels: 89.3 us -> 84.5 us
    pallas_call x1, Pallas kernels: 89.3 us -> 84.5 us  [per_device(): pl.pallas_call(functools.partial(kernel, n), out_shape=(image, image), in...]
where the time goes in v4:
time: 88.5 us; the launch traced here: 88.3 us
  Pallas kernels  84.5 us (95%)
  local copies, waits for them, and re-layouts  3.23 us (4%)
    pallas_call x1, Pallas kernels, per_device(): pl.pallas_call(functools.partial(kernel, n), out_shape=(image, image), in...  84.5 us
    unnamed x2, local copies, waits for them, and re-layouts  3.23 us

profile of v4, /device:TPU:8, one launch (start us, length us, event | category | flops | bytes accessed | tf_op | source)
XLA Modules:
  0.0 88.3 jit_solution(2417619491339772469)
XLA Ops:
  0.6 84.5 %shard_map.113 = (f32[3,1,128,128]{3,2,1,0:T(8,128)}, f32[3,1,128,128]{3,2,1,0:T(8,128)}) custom-call(f32[3,1,128,128]{3,2,1,0:T(8,128)} %pol_hbm.1, f32[1,128,128]{2,1,0:T(8,128)} %inv_hbm.1, s32[1,16,16]{2,1,0:T(8,128)} %occ_hbm.1, f32[6,2,256,256]{3,2,1,0:T(8,128)} %green_hbm.1, bf16[512,256]{1,0:T(8,128)(2,1)} %constant.12.clone.wh_hbm, ...), custom_call_target="tpu_custom_call" | custom-call | tf_op jit(solution)/shard_map/pallas_call | solution.py:351
  85.1 1.6 %copy.14 = f32[3,1,128,128]{3,2,1,0:T(8,128)} copy(f32[3,1,128,128]{3,2,1,0:T(8,128)} %get-tuple-element.4) | data formatting | bytes 393216
  86.7 1.6 %copy.15 = f32[3,1,128,128]{3,2,1,0:T(8,128)} copy(f32[3,1,128,128]{3,2,1,0:T(8,128)} %get-tuple-element.5) | data formatting | bytes 393216

commit v5 on v4

--- a/solution.py
+++ b/solution.py
@@ -13,6 +13,7 @@
 MESH = pl.DeviceIdType.MESH
 ROW = 16
 RING = 8
+SIDE = 4
 REACH = 4
 
 
@@ -50,7 +51,7 @@
     own_p, side_p, own_q, side_q,
     slab_in, part_out, part_in,
     own_s, side_s, recv, back_s, own_b, side_b,
-    fwd_send, fwd_recv, back_send, back_recv, slab_send, slab_recv, part_send, part_recv, first_sem, later_sem, out_sem,
+    fwd_send, fwd_recv, back_send, back_recv, slab_send, slab_recv, part_send, part_recv, first_sem, later_sem, out_sem, met,
 ):
     me = lax.axis_index("slab")
     row, rank = me // ROW, lax.rem(me, ROW)
@@ -69,19 +70,25 @@
 
     barrier = pltpu.get_barrier_semaphore()
 
-    def greet(target):
-        pl.semaphore_signal(barrier, inc=1, device_id={"slab": target}, device_id_type=MESH)
-
-    for k in range(REACH - 1, 0, -1):
-
-        @pl.loop(0, ROW, unroll=4)
-        def _(r):
-            greet(at(row + k, r))
-            greet(at(row - k, r))
-
-    @pl.loop(1, ROW, unroll=3)
-    def _(i):
-        greet(row * ROW + (rank ^ i))
+    y, x = rank // SIDE, lax.rem(rank, SIDE)
+
+    def chip(dz, dy, dx):
+        to_y, to_x = lax.rem(y + dy + SIDE, SIDE), lax.rem(x + dx + SIDE, SIDE)
+        return at(row + dz, to_y * SIDE + to_x)
+
+    def greet(sem, targets):
+        for shift in targets:
+            pl.semaphore_signal(
+                sem, inc=1, device_id={"slab": chip(*shift)}, device_id_type=MESH
+            )
+
+    def heard(sem, targets):
+        pl.semaphore_wait(sem, len(targets))
+
+    around = [(d, 0, 0) for d in (1, -1)] + [(0, d, 0) for d in (1, -1)] + [(0, 0, d) for d in (1, -1)]
+    ring = [(1, 0, 0), (-1, 0, 0), (0, 0, 1), (0, 0, 2), (0, 0, 3)]
+    column = [(d, 0, 0) for d in (3, -3, 2, -2, 1, -1)]
+    greet(barrier, around)
 
     first = [
         pltpu.make_async_copy(src, dst, first_sem.at[i])
@@ -99,6 +106,8 @@
         copy.start()
     for copy in first:
         copy.wait()
+    heard(barrier, around)
+    greet(met.at[0], around)
 
     blocks = occ.shape[1]
     each = cells // blocks
@@ -114,7 +123,124 @@
     for c in range(3):
         field[c] = pol[c, 0].T * mask_t[...]
 
+    def slab_copy(turn, c, side):
+        return pltpu.make_async_remote_copy(
+            src_ref=field.at[turn * 3 + c],
+            dst_ref=slab_in.at[turn, side, c],
+            send_sem=slab_send.at[turn, side, c],
+            recv_sem=slab_recv.at[turn, side, c],
+            device_id={"slab": sides[1 - side]},
+            device_id_type=MESH,
+        )
+
+    def part_copy(turn, a, side):
+        return pltpu.make_async_remote_copy(
+            src_ref=part_out.at[turn, side, a],
+            dst_ref=part_in.at[turn, side, a],
+            send_sem=part_send.at[turn, side, a],
+            recv_sem=part_recv.at[turn, side, a],
+            device_id={"slab": sides[side]},
+            device_id_type=MESH,
+        )
+
+    def out_copy(turn, a):
+        out = (out_0, out_1)[turn]
+        return pltpu.make_async_copy(images.at[turn, a], out.at[a, 0], out_sem.at[turn, a])
+
+    def send_to(src, dst, target, send_sem, recv_sem):
+        pltpu.make_async_remote_copy(
+            src_ref=src, dst_ref=dst, send_sem=send_sem, recv_sem=recv_sem,
+            device_id={"slab": target}, device_id_type=MESH,
+        ).start()
+
+    def messages(own, side):
+        @pl.loop(0, ROW // 2, unroll=2)
+        def _(i):
+            even = 2 * i + lax.rem(rank, 2)
+            side(0, REACH - 1, even)
+            side(1, REACH - 1, even ^ 1)
+
+        for k in range(REACH - 2, 0, -1):
+
+            @pl.loop(0, ROW, unroll=4)
+            def _(r):
+                side(0, k, r)
+                side(1, k, r)
+
+        @pl.loop(1, ROW, unroll=3)
+        def _(i):
+            r = rank ^ i
+            side(0, 0, r)
+            side(1, 0, r)
+            own(r)
+
+    def forward(slot, low, width, sem):
+        sems = (fwd_send.at[sem], fwd_recv.at[sem])
+        span = pl.ds(low, width)
+
+        def own(r):
+            send_to(
+                own_s.at[slot, span, pl.ds(r, 1), :], recv.at[slot, span, pl.ds(me, 1), :],
+                row * ROW + r, *sems,
+            )
+
+        def side(which, k, r):
+            send_to(
+                side_s.at[slot, which, span, pl.ds(k * ROW + r, 1), :],
+                recv.at[slot, span, pl.ds(sides[which], 1), :],
+                at(row + step_of[which] * k, r), *sems,
+            )
+
+        messages(own, side)
+        recv[slot, span, pl.ds(me, 1), :] = own_s[slot, span, pl.ds(rank, 1), :]
+        for which in range(2):
+            recv[slot, span, pl.ds(sides[which], 1), :] = side_s[
+                slot, which, span, pl.ds(rank, 1), :
+            ]
+
+    def backward(slot, low, width, sem):
+        sems = (back_send.at[sem], back_recv.at[sem])
+        span = pl.ds(low, width)
+
+        def own(r):
+            send_to(
+                back_s.at[slot, span, pl.ds(row * ROW + r, 1), :],
+                own_b.at[slot, span, pl.ds(rank, 1), :],
+                row * ROW + r, *sems,
+            )
+
+        def side(which, k, r):
+            collector = row - step_of[which] * k
+            send_to(
+                back_s.at[slot, span, pl.ds(at(collector - step_of[which], r), 1), :],
+                side_b.at[slot, which, span, pl.ds(k * ROW + rank, 1), :],
+                at(collector, r), *sems,
+            )
+
+        messages(own, side)
+        own_b[slot, span, pl.ds(rank, 1), :] = back_s[slot, span, pl.ds(me, 1), :]
+        for which in range(2):
+            side_b[slot, which, span, pl.ds(rank, 1), :] = back_s[
+                slot, span, pl.ds(sides[which], 1), :
+            ]
+
+    def wait_for(ref, width, sem):
+        bytes_of = ref.at[0, pl.ds(0, width), pl.ds(0, n - 3), :]
+        pltpu.make_async_copy(bytes_of, bytes_of, sem).wait()
+
+    fwd_plan = ((0, 0, 2), (0, 2, 2), (0, 4, 2), (1, 0, 6))
+    back_plan = ((0, 0, 6), (1, 0, 2), (1, 2, 2), (1, 4, 2))
+
+    for c in range(3):
+        for side in range(2):
+            slab_copy(0, c, side).start()
+    heard(met.at[0], around)
+    greet(met.at[1], ring)
+
     for half, table in enumerate((ph, plo)):
+        if half == 1:
+            heard(met.at[1], ring)
+            greet(met.at[2], column)
         pick = pl.ds(pl.multiple_of(row * ROW, ROW), ROW)
         own_p[half] = table[:, pick, :]
         own_q[half] = own_p[half].astype(F32).reshape(4 * ROW, cells).T.astype(BF16)
@@ -125,119 +251,7 @@
             side_q[half, side] = (
                 side_p[half, side].astype(F32).reshape(4 * REACH * ROW, cells).T.astype(BF16)
             )
-
-    def slab_copy(turn, c, side):
-        return pltpu.make_async_remote_copy(
-            src_ref=field.at[turn * 3 + c],
-            dst_ref=slab_in.at[turn, side, c],
-            send_sem=slab_send.at[turn, side, c],
-            recv_sem=slab_recv.at[turn, side, c],
-            device_id={"slab": sides[1 - side]},
-            device_id_type=MESH,
-        )
-
-    def part_copy(turn, a, side):
-        return pltpu.make_async_remote_copy(
-            src_ref=part_out.at[turn, side, a],
-            dst_ref=part_in.at[turn, side, a],
-            send_sem=part_send.at[turn, side, a],
-            recv_sem=part_recv.at[turn, side, a],
-            device_id={"slab": sides[side]},
-            device_id_type=MESH,
-        )
-
-    def out_copy(turn, a):
-        out = (out_0, out_1)[turn]
-        return pltpu.make_async_copy(images.at[turn, a], out.at[a, 0], out_sem.at[turn, a])
-
-    def send_to(src, dst, target, send_sem, recv_sem):
-        pltpu.make_async_remote_copy(
-            src_ref=src, dst_ref=dst, send_sem=send_sem, recv_sem=recv_sem,
-            device_id={"slab": target}, device_id_type=MESH,
-        ).start()
-
-    def messages(own, side):
-        @pl.loop(0, ROW // 2, unroll=2)
-        def _(i):
-            even = 2 * i + lax.rem(rank, 2)
-            side(0, REACH - 1, even)
-            side(1, REACH - 1, even ^ 1)
-
-        for k in range(REACH - 2, 0, -1):
-
-            @pl.loop(0, ROW, unroll=4)
-            def _(r):
-                side(0, k, r)
-                side(1, k, r)
-
-        @pl.loop(1, ROW, unroll=3)
-        def _(i):
-            r = rank ^ i
-            side(0, 0, r)
-            side(1, 0, r)
-            own(r)
-
-    def forward(slot, low, width, sem):
-        sems = (fwd_send.at[sem], fwd_recv.at[sem])
-        span = pl.ds(low, width)
-
-        def own(r):
-            send_to(
-                own_s.at[slot, span, pl.ds(r, 1), :], recv.at[slot, span, pl.ds(me, 1), :],
-                row * ROW + r, *sems,
-            )
-
-        def side(which, k, r):
-            send_to(
-                side_s.at[slot, which, span, pl.ds(k * ROW + r, 1), :],
-                recv.at[slot, span, pl.ds(sides[which], 1), :],
-                at(row + step_of[which] * k, r), *sems,
-            )
-
-        messages(own, side)
-        recv[slot, span, pl.ds(me, 1), :] = own_s[slot, span, pl.ds(rank, 1), :]
-        for which in range(2):
-            recv[slot, span, pl.ds(sides[which], 1), :] = side_s[
-                slot, which, span, pl.ds(rank, 1), :
-            ]
-
-    def backward(slot, low, width, sem):
-        sems = (back_send.at[sem], back_recv.at[sem])
-        span = pl.ds(low, width)
-
-        def own(r):
-            send_to(
-                back_s.at[slot, span, pl.ds(row * ROW + r, 1), :],
-                own_b.at[slot, span, pl.ds(rank, 1), :],
-                row * ROW + r, *sems,
-            )
-
-        def side(which, k, r):
-            collector = row - step_of[which] * k
-            send_to(
-                back_s.at[slot, span, pl.ds(at(collector - step_of[which], r), 1), :],
-                side_b.at[slot, which, span, pl.ds(k * ROW + rank, 1), :],
-                at(collector, r), *sems,
-            )
-
-        messages(own, side)
-        own_b[slot, span, pl.ds(rank, 1), :] = back_s[slot, span, pl.ds(me, 1), :]
-        for which in range(2):
-            side_b[slot, which, span, pl.ds(rank, 1), :] = back_s[
-                slot, span, pl.ds(sides[which], 1), :
-            ]
-
-    def wait_for(ref, width, sem):
-        bytes_of = ref.at[0, pl.ds(0, width), pl.ds(0, n - 3), :]
-        pltpu.make_async_copy(bytes_of, bytes_of, sem).wait()
-
-    fwd_plan = ((0, 0, 2), (0, 2, 2), (0, 4, 2), (1, 0, 6))
-    back_plan = ((0, 0, 6), (1, 0, 2), (1, 2, 2), (1, 4, 2))
-
-    pl.semaphore_wait(barrier, (2 * REACH - 1) * ROW - 1)
-    for c in range(3):
-        for side in range(2):
-            slab_copy(0, c, side).start()
+    heard(met.at[2], column)
 
     scale = 1.0 / (8 * cells * cells * n)
 
@@ -376,6 +390,7 @@
             pltpu.VMEM((4, 2, 6, span, cells), F32),
             dma((8,)), dma((8,)), dma((8,)), dma((8,)),
             dma((2, 2, 3)), dma((2, 2, 3)), dma((2, 2, 3)), dma((2, 2, 3)), dma((5,)), dma((5,)), dma((2, 3)),
+            pltpu.SemaphoreType.REGULAR((3,)),
         ],
         compiler_params=pltpu.CompilerParams(
             has_side_effects=True, collective_id=0, vmem_limit_bytes=56 * 2**20

time: 88.5 us -> 86.3 us (0.975)
  Pallas kernels: 84.5 us -> 82.3 us
    pallas_call x1, Pallas kernels: 84.5 us -> 82.3 us  [per_device(): pl.pallas_call(functools.partial(kernel, n), out_shape=(image, image), in...]
where the time goes in v5:
time: 86.3 us; the launch traced here: 86.2 us
  Pallas kernels  82.3 us (95%)
  local copies, waits for them, and re-layouts  3.23 us (4%)
    pallas_call x1, Pallas kernels, per_device(): pl.pallas_call(functools.partial(kernel, n), out_shape=(image, image), in...  82.3 us
    unnamed x2, local copies, waits for them, and re-layouts  3.23 us

profile of v5, /device:TPU:8, one launch (start us, length us, event | category | flops | bytes accessed | tf_op | source)
XLA Modules:
  0.0 86.2 jit_solution(17400024616034374886)
XLA Ops:
  0.6 82.3 %shard_map.113 = (f32[3,1,128,128]{3,2,1,0:T(8,128)}, f32[3,1,128,128]{3,2,1,0:T(8,128)}) custom-call(f32[3,1,128,128]{3,2,1,0:T(8,128)} %pol_hbm.1, f32[1,128,128]{2,1,0:T(8,128)} %inv_hbm.1, s32[1,16,16]{2,1,0:T(8,128)} %occ_hbm.1, f32[6,2,256,256]{3,2,1,0:T(8,128)} %green_hbm.1, bf16[512,256]{1,0:T(8,128)(2,1)} %constant.12.clone.wh_hbm, ...), custom_call_target="tpu_custom_call" | custom-call | tf_op jit(solution)/shard_map/pallas_call | solution.py:365
  83.0 1.6 %copy.14 = f32[3,1,128,128]{3,2,1,0:T(8,128)} copy(f32[3,1,128,128]{3,2,1,0:T(8,128)} %get-tuple-element.4) | data formatting | bytes 393216
  84.6 1.6 %copy.15 = f32[3,1,128,128]{3,2,1,0:T(8,128)} copy(f32[3,1,128,128]{3,2,1,0:T(8,128)} %get-tuple-element.5) | data formatting | bytes 393216

commit v6 on v5

--- a/solution.py
+++ b/solution.py
@@ -280,22 +280,25 @@
 
         for kzb, slot in enumerate(slots):
             for sem, (plane, low, width) in enumerate(fwd_plan):
-                if plane == kzb:
-                    wait_for(recv, width, fwd_recv.at[4 * turn + sem])
-            rows = split(
-                jnp.concatenate(
-                    [recv[slot, 2 * c : 2 * c + 2].reshape(half, cells) for c in range(3)], axis=1
+                if plane != kzb:
+                    continue
+                wait_for(recv, width, fwd_recv.at[4 * turn + sem])
+                components = range(low // 2, (low + width) // 2)
+                rows = split(
+                    jnp.concatenate(
+                        [recv[slot, 2 * c : 2 * c + 2].reshape(half, cells) for c in components],
+                        axis=1,
+                    )
                 )
-            )
-            for part in range(2):
-                at_rows = slice(part * half, (part + 1) * half)
-                product = dot3((wh[at_rows], wl[at_rows]), rows)
-                for c in range(3):
-                    over_x[c, :, part * cells : (part + 1) * cells] = product[
-                        :, c * cells : (c + 1) * cells
-                    ]
-            for c in range(3):
-                spectrum[c] = dot3(split(over_x[c]), (th[...], tl[...]))
+                for part in range(2):
+                    at_rows = slice(part * half, (part + 1) * half)
+                    product = dot3((wh[at_rows], wl[at_rows]), rows)
+                    for i, c in enumerate(components):
+                        over_x[c, :, part * cells : (part + 1) * cells] = product[
+                            :, i * cells : (i + 1) * cells
+                        ]
+                for c in components:
+                    spectrum[c] = dot3(split(over_x[c]), (th[...], tl[...]))
             for a, combo in enumerate(((0, 3, 4), (3, 1, 5), (4, 5, 2))):
                 parts = [
                     green[combo[0], kzb] * spectrum[0, :, k : k + half]

time: 86.3 us -> 84.2 us (0.976)
  Pallas kernels: 82.3 us -> 80 us
    pallas_call x1, Pallas kernels: 82.3 us -> 80 us  [per_device(): pl.pallas_call(functools.partial(kernel, n), out_shape=(image, image), in...]
where the time goes in v6:
time: 84.2 us; the launch traced here: 83.9 us
  Pallas kernels  80 us (95%)
  local copies, waits for them, and re-layouts  3.23 us (4%)
    pallas_call x1, Pallas kernels, per_device(): pl.pallas_call(functools.partial(kernel, n), out_shape=(image, image), in...  80 us
    unnamed x2, local copies, waits for them, and re-layouts  3.23 us

profile of v6, /device:TPU:8, one launch (start us, length us, event | category | flops | bytes accessed | tf_op | source)
XLA Modules:
  0.0 83.9 jit_solution(6420358235048276894)
XLA Ops:
  0.6 80.0 %shard_map.113 = (f32[3,1,128,128]{3,2,1,0:T(8,128)}, f32[3,1,128,128]{3,2,1,0:T(8,128)}) custom-call(f32[3,1,128,128]{3,2,1,0:T(8,128)} %pol_hbm.1, f32[1,128,128]{2,1,0:T(8,128)} %inv_hbm.1, s32[1,16,16]{2,1,0:T(8,128)} %occ_hbm.1, f32[6,2,256,256]{3,2,1,0:T(8,128)} %green_hbm.1, bf16[512,256]{1,0:T(8,128)(2,1)} %constant.12.clone.wh_hbm, ...), custom_call_target="tpu_custom_call" | custom-call | tf_op jit(solution)/shard_map/pallas_call | solution.py:368
  80.7 1.6 %copy.14 = f32[3,1,128,128]{3,2,1,0:T(8,128)} copy(f32[3,1,128,128]{3,2,1,0:T(8,128)} %get-tuple-element.4) | data formatting | bytes 393216
  82.3 1.6 %copy.15 = f32[3,1,128,128]{3,2,1,0:T(8,128)} copy(f32[3,1,128,128]{3,2,1,0:T(8,128)} %get-tuple-element.5) | data formatting | bytes 393216

commit v7 on v6

--- a/solution.py
+++ b/solution.py
@@ -104,7 +104,7 @@
     ]
     for copy in (*first, *later):
         copy.start()
-    for copy in first:
+    for copy in first[:2]:
         copy.wait()
     heard(barrier, around)
     greet(met.at[0], around)
@@ -119,7 +119,6 @@
     mask_t[...] = lax.dot_general(
         spread, rows, (((1,), (1,)), ((), ())), preferred_element_type=F32
     )
-    inv_t[...] = inv[0].T
     for c in range(3):
         field[c] = pol[c, 0].T * mask_t[...]
 
@@ -236,6 +235,9 @@
             slab_copy(0, c, side).start()
     heard(met.at[0], around)
     greet(met.at[1], ring)
+    for copy in first[2:]:
+        copy.wait()
+    inv_t[...] = inv[0].T
 
     for half, table in enumerate((ph, plo)):
         if half == 1:
@@ -299,6 +301,7 @@
                         ]
                 for c in components:
                     spectrum[c] = dot3(split(over_x[c]), (th[...], tl[...]))
+            stacked = []
             for a, combo in enumerate(((0, 3, 4), (3, 1, 5), (4, 5, 2))):
                 parts = [
                     green[combo[0], kzb] * spectrum[0, :, k : k + half]
@@ -308,12 +311,19 @@
                 ]
                 over_y = dot3(split(jnp.concatenate(parts, axis=1)), (wh[...], wl[...]))
                 both = jnp.concatenate([over_y[:, :cells], over_y[:, cells:]], axis=0)
+                if kzb == 0:
+                    stacked.append(both)
+                    continue
                 back_s[slot, 2 * a : 2 * a + 2] = dot3((th[...], tl[...]), split(both)).reshape(
                     2, n, cells
                 )
-                if kzb == 1:
-                    backward(slot, 2 * a, 2, 4 * turn + 1 + a)
+                backward(slot, 2 * a, 2, 4 * turn + 1 + a)
             if kzb == 0:
+                product = dot3((th[...], tl[...]), split(jnp.concatenate(stacked, axis=1)))
+                for a in range(3):
+                    back_s[slot, 2 * a : 2 * a + 2] = product[
+                        :, a * cells : (a + 1) * cells
+                    ].reshape(2, n, cells)
                 backward(slot, 0, 6, 4 * turn)
 
         wait_for(recv, 6, back_recv.at[4 * turn])

time: 84.2 us -> 83.7 us (level)
  no operation moved by 1% of the time
where the time goes in v7:
time: 83.7 us; the launch traced here: 83.6 us
  Pallas kernels  79.7 us (95%)
  local copies, waits for them, and re-layouts  3.23 us (4%)
    pallas_call x1, Pallas kernels, per_device(): pl.pallas_call(functools.partial(kernel, n), out_shape=(image, image), in...  79.7 us
    unnamed x2, local copies, waits for them, and re-layouts  3.23 us

profile of v7, /device:TPU:8, one launch (start us, length us, event | category | flops | bytes accessed | tf_op | source)
XLA Modules:
  0.0 83.6 jit_solution(16990213191785240779)
XLA Ops:
  0.6 79.7 %shard_map.113 = (f32[3,1,128,128]{3,2,1,0:T(8,128)}, f32[3,1,128,128]{3,2,1,0:T(8,128)}) custom-call(f32[3,1,128,128]{3,2,1,0:T(8,128)} %pol_hbm.1, f32[1,128,128]{2,1,0:T(8,128)} %inv_hbm.1, s32[1,16,16]{2,1,0:T(8,128)} %occ_hbm.1, f32[6,2,256,256]{3,2,1,0:T(8,128)} %green_hbm.1, bf16[512,256]{1,0:T(8,128)(2,1)} %constant.12.clone.wh_hbm, ...), custom_call_target="tpu_custom_call" | custom-call | tf_op jit(solution)/shard_map/pallas_call | solution.py:378
  80.4 1.6 %copy.14 = f32[3,1,128,128]{3,2,1,0:T(8,128)} copy(f32[3,1,128,128]{3,2,1,0:T(8,128)} %get-tuple-element.4) | data formatting | bytes 393216
  82.0 1.6 %copy.15 = f32[3,1,128,128]{3,2,1,0:T(8,128)} copy(f32[3,1,128,128]{3,2,1,0:T(8,128)} %get-tuple-element.5) | data formatting | bytes 393216
